TPU v7x, 32 devices: a whole 2x2x4 slice. The times are simulated.
32 devices in a mesh: gx: 8 (over y, x, core), gy: 4 (over z).
Axes of the slice: x: 2, y: 2, z: 4, core: 2. Of those that a mesh axis runs over, the one named last changes fastest.
Arguments:
- u_old: float32 [3, 256, 128, 256], P(None, 'gx', 'gy'), may hold values from -0.6 to 0.6
- density: float32 [256, 128, 256], P('gx', 'gy'), may hold values from 0.5 to 2
- offsets: float32 [3, 512, 128], P(None, ('gx', 'gy')), may hold values from 0 to 1
- forces: float32 [3, 512, 128], P(None, ('gx', 'gy')), may hold values from -60 to 60
- base_x: int32 [512, 128], P(('gx', 'gy')), may hold values from 0 to 31
- base_y: int32 [512, 128], P(('gx', 'gy')), may hold values from 0 to 31
- base_z: int32 [512, 128], P(('gx', 'gy')), may hold values from 0 to 255
- tile_count: int32 [32], P(('gx', 'gy')), may hold values from 1 to 16, as said below
Outputs:
- u_new: float32 [3, 256, 128, 256], P(None, 'gx', 'gy')
- marker_velocity: float32 [3, 512, 128], P(None, ('gx', 'gy'))
Inputs may be any that keep to these rules, and one draw needn't show every extreme that they name: `tile_count`: every draw has a device with exactly 16 live tiles; loads are skewed, with a mean near a quarter of that.
All inputs are finite; a program needn't handle non-finite values.
Results may differ from a plain program's by a relative error of at most 0.000075.
Values sent between devices are 32-bit elements; how exact they have to be, the bound alone decides.
A program may use at most 64 MiB of HBM per device.

v0:
```python
import functools

import jax
import jax.numpy as jnp
from jax import lax
from jax.experimental import pallas as pl
from jax.experimental.pallas import tpu as pltpu
from jax.sharding import PartitionSpec as P

VMEM_LIMIT = 60 * 1024 * 1024
SEND_LIMIT = 10 * 1024 * 1024
MAIN_LIMIT = 35 * 1024 * 1024


def divisor(count, most):
    return max(d for d in range(1, most + 1) if count % d == 0)


def moved(value, step_x, step_y):
    if step_y == 0:
        n = lax.axis_size("gx")
        return lax.ppermute(value, "gx", [(i, (i + step_x) % n) for i in range(n)])
    if step_x == 0:
        n = lax.axis_size("gy")
        return lax.ppermute(value, "gy", [(i, (i + step_y) % n) for i in range(n)])
    nx, ny = lax.axis_size("gx"), lax.axis_size("gy")
    pairs = [
        (i * ny + j, ((i + step_x) % nx) * ny + (j + step_y) % ny)
        for i in range(nx)
        for j in range(ny)
    ]
    return lax.ppermute(value, ("gx", "gy"), pairs)


def stencil(frac):
    root = jnp.sqrt(1.0 + 4.0 * frac - 4.0 * frac * frac)
    return [
        (3.0 - 2.0 * frac - root) / 8.0,
        (3.0 - 2.0 * frac + root) / 8.0,
        (1.0 + 2.0 * frac + root) / 8.0,
        (1.0 + 2.0 * frac - root) / 8.0,
    ]


def pick(delta, four):
    total = jnp.where(delta == 0, four[0], 0.0)
    for k in range(1, 4):
        total = jnp.where(delta == k, four[k], total)
    return total


def wrapped(delta, length):
    delta = jnp.where(delta < 0, delta + length, delta)
    return jnp.where(delta >= length, delta - length, delta)


def edge_weights(frac, base, rows, size):
    row = lax.broadcasted_iota(jnp.int32, (rows, base.shape[1]), 0)
    cell = jnp.where(row == size + 2, -1, row)
    cell = jnp.where(row > size + 2, -8, cell)
    return pick(cell - base + 1, stencil(frac))


def halves(value):
    high = value.astype(jnp.bfloat16)
    low = (value - high.astype(jnp.float32)).astype(jnp.bfloat16)
    return high, low


def edges(size):
    return (size - 1, size, size + 1), (size + 2, 0, 1)


def spread_kernel(size_x, size_y, feat, base, grid, *refs):
    slabs, (wx_s, wy_s, high_s, low_s) = refs[:8], refs[8:]
    planes, rows, depth = grid.shape[1], grid.shape[2], grid.shape[3]
    markers = feat.shape[1]
    wx_s[...] = edge_weights(feat[0:1, :], base[0:1, :], wx_s.shape[0], size_x)
    wy_s[...] = edge_weights(feat[1:2, :], base[1:2, :], rows, size_y)
    four = stencil(feat[2:3, :])
    column = jnp.concatenate(
        four + [base[2:3, :].astype(jnp.float32)] + [feat[3 + c : 4 + c, :] for c in range(3)], axis=0
    ).T
    cut = 256 if markers % 256 == 0 else 128
    for start in range(0, markers, cut):
        part = column[start : start + cut]
        lane = lax.broadcasted_iota(jnp.int32, (cut, depth), 1)
        delta = wrapped(lane - part[:, 4:5].astype(jnp.int32) + 1, depth)
        wz = pick(delta, [part[:, k : k + 1] for k in range(4)])
        for c in range(3):
            high, low = halves(wz * part[:, 5 + c : 6 + c])
            high_s[start : start + cut, c * depth : (c + 1) * depth] = high
            low_s[start : start + cut, c * depth : (c + 1) * depth] = low
    group = divisor(planes, 8)

    def turn(g, carry):
        first = g * group
        left = jnp.concatenate(
            [wy_s[...] * wx_s[pl.ds(first + j, 1), :] for j in range(group)], axis=0
        )
        high, low = halves(left)
        dot = functools.partial(jnp.dot, preferred_element_type=jnp.float32)
        total = dot(high, high_s[...]) + dot(low, high_s[...]) + dot(high, low_s[...])
        for j in range(group):
            for c in range(3):
                grid[c, first + j] = total[j * rows : (j + 1) * rows, c * depth : (c + 1) * depth]
        return carry

    lax.fori_loop(0, planes // group, turn, 0)
    sides_x, sides_y = edges(size_x), edges(size_y)
    for side in range(2):
        for c in range(3):
            for j, p in enumerate(sides_x[side]):
                slabs[side][c, j] = grid[c, p]
                for other in range(2):
                    for i, r in enumerate(sides_y[other]):
                        slabs[4 + 2 * side + other][c, j, i : i + 1] = grid[c, p, r : r + 1]
            for i, r in enumerate(sides_y[side]):
                for p in range(planes):
                    slabs[2 + side][c, i, p : p + 1] = grid[c, p, r : r + 1]


def read_kernel(size_x, size_y, time_step, *refs):
    feat, base, grid, u_old, density, low_x, high_x, low_y, high_y = refs[:9]
    slabs, (u_new, velocity) = refs[9:17], refs[17:19]
    total, wx_s, wy_s, wz3, table = refs[19:]
    planes, rows, depth = grid.shape[1], grid.shape[2], grid.shape[3]
    markers = feat.shape[1]
    wx_s[...] = edge_weights(feat[0:1, :], base[0:1, :], wx_s.shape[0], size_x)
    wy_s[...] = edge_weights(feat[1:2, :], base[1:2, :], rows, size_y)
    cut = 256 if markers % 256 == 0 else 128
    for start in range(0, markers, cut):
        at = slice(start, start + cut)
        row = lax.broadcasted_iota(jnp.int32, (depth, cut), 0)
        delta = wrapped(row - base[2:3, at] + 1, depth)
        high, low = halves(pick(delta, stencil(feat[2:3, at])))
        wz3[0:depth, at] = high
        wz3[depth : 2 * depth, at] = high
        wz3[2 * depth :, at] = low
    total[...] = grid[...]
    near_x, near_y = edges(size_x)[::-1], edges(size_y)[::-1]
    for side in range(2):
        for c in range(3):
            for j, p in enumerate(near_x[side]):
                total[c, p] = total[c, p] + slabs[side][c, j]
                for other in range(2):
                    for i, r in enumerate(near_y[other]):
                        total[c, p, r : r + 1] = (
                            total[c, p, r : r + 1] + slabs[4 + 2 * side + other][c, j, i : i + 1]
                        )
            for i, r in enumerate(near_y[side]):
                for p in range(planes):
                    total[c, p, r : r + 1] = total[c, p, r : r + 1] + slabs[2 + side][c, i, p : p + 1]
    group = divisor(planes, 6)
    spare = jnp.ones((rows - size_y - 3, depth), jnp.float32)

    def plane_state(k, p):
        if p < size_x:
            main = density[p] if k == 3 else u_old[k, p]
        elif p < size_x + 2:
            main = high_x[k, p - size_x]
        else:
            main = low_x[k, 0]
        edge = [high_y[k, 0, p : p + 1], high_y[k, 1, p : p + 1], low_y[k, 0, p : p + 1], spare]
        return jnp.concatenate([main] + edge, axis=0)

    for g in range(planes // group):
        pieces = []
        for p in range(g * group, (g + 1) * group):
            scale = time_step / plane_state(3, p)
            for c in range(3):
                value = plane_state(c, p) + total[c, p] * scale
                if p < size_x:
                    u_new[c, p] = value[:size_y]
                pieces.append(value)
        high, low = halves(jnp.concatenate(pieces, axis=0))
        table[g, :, 0:depth] = high
        table[g, :, depth : 2 * depth] = low
        table[g, :, 2 * depth :] = high

    def turn(step, carry):
        at = pl.ds(pl.multiple_of(step * cut, cut), cut)
        right = wz3[:, at]
        wy = wy_s[:, at]
        sums = [jnp.zeros((8, cut), jnp.float32) for _ in range(3)]
        for g in range(planes // group):
            found = jnp.dot(table[g], right, preferred_element_type=jnp.float32)
            for j in range(group):
                p = g * group + j
                weight = wy * wx_s[p : p + 1, at]
                for c in range(3):
                    first = (j * 3 + c) * rows
                    product = found[first : first + rows] * weight
                    for r in range(0, rows, 8):
                        sums[c] = sums[c] + product[r : r + 8]
        velocity[:, at] = (
            jnp.concatenate([jnp.sum(s, axis=0, keepdims=True) for s in sums], axis=0) * feat[6:7, at]
        )
        return carry

    lax.fori_loop(0, markers // cut, turn, 0)


def dense_device(u_old, density, offsets, forces, base_x, base_y, base_z, tile_count):
    time_step = 0.5
    _, size_x, size_y, depth = u_old.shape
    slots, width = base_x.shape
    markers = slots * width
    planes = size_x + 3
    rows = -(-(size_y + 3) // 8) * 8
    lines = -(-planes // 8) * 8
    f32, bf16 = jnp.float32, jnp.bfloat16
    live = (lax.broadcasted_iota(jnp.int32, (slots, width), 0) < tile_count[0]).astype(f32)
    feat = jnp.concatenate([offsets, forces * live[None], live[None]], axis=0).reshape(7, markers)
    base = jnp.stack([base_x, base_y, base_z], axis=0).reshape(3, markers)

    up = jnp.concatenate([u_old[:, size_x - 1 :], density[None, size_x - 1 :]], axis=0)
    down = jnp.concatenate([u_old[:, :2], density[None, :2]], axis=0)
    low_x, high_x = moved(up, 1, 0), moved(down, -1, 0)

    def strip(r):
        inner = jnp.concatenate([u_old[:, :, r], density[None, :, r]], axis=0)
        return jnp.concatenate([inner, high_x[:, :, r], low_x[:, :, r]], axis=1)

    low_y = moved(strip(size_y - 1)[:, None], 0, 1)
    high_y = moved(jnp.stack([strip(0), strip(1)], axis=1), 0, -1)

    params = pltpu.CompilerParams(vmem_limit_bytes=VMEM_LIMIT)
    slab_x = jax.ShapeDtypeStruct((3, 3, rows, depth), f32)
    slab_y = jax.ShapeDtypeStruct((3, 3, planes, depth), f32)
    corner = jax.ShapeDtypeStruct((3, 3, 3, depth), f32)
    whole = pl.BlockSpec(memory_space=pltpu.VMEM)
    flops = 6 * planes * rows * 3 * depth * markers
    cost = pl.CostEstimate(flops=flops, transcendentals=0, bytes_accessed=8 * planes * rows * depth)
    grid, *slabs = pl.pallas_call(
        functools.partial(spread_kernel, size_x, size_y),
        out_shape=[jax.ShapeDtypeStruct((3, planes, rows, depth), f32)]
        + [slab_x] * 2
        + [slab_y] * 2
        + [corner] * 4,
        in_specs=[whole] * 2,
        out_specs=[whole] * 9,
        scratch_shapes=[
            pltpu.VMEM((lines, markers), f32),
            pltpu.VMEM((rows, markers), f32),
            pltpu.VMEM((markers, 3 * depth), bf16),
            pltpu.VMEM((markers, 3 * depth), bf16),
        ],
        compiler_params=params,
        cost_estimate=cost,
        name="spread",
    )(feat, base)
    ways = [(1, 0), (-1, 0), (0, 1), (0, -1), (1, 1), (1, -1), (-1, 1), (-1, -1)]
    slabs = [moved(slab, *way) for slab, way in zip(slabs, ways)]
    group = divisor(planes, 6)
    u_new, velocity = pl.pallas_call(
        functools.partial(read_kernel, size_x, size_y, time_step),
        out_shape=[
            jax.ShapeDtypeStruct(u_old.shape, f32),
            jax.ShapeDtypeStruct((3, markers), f32),
        ],
        in_specs=[whole] * 17,
        out_specs=[whole] * 2,
        scratch_shapes=[
            pltpu.VMEM((3, planes, rows, depth), f32),
            pltpu.VMEM((lines, markers), f32),
            pltpu.VMEM((rows, markers), f32),
            pltpu.VMEM((3 * depth, markers), bf16),
            pltpu.VMEM((planes // group, group * 3 * rows, 3 * depth), bf16),
        ],
        compiler_params=params,
        cost_estimate=cost,
        name="read",
    )(feat, base, grid, u_old, density, low_x, high_x, low_y, high_y, *slabs)
    return (u_new, velocity.reshape(3, slots, width))


MESH = pl.DeviceIdType.MESH
WAYS = [(1, 0), (-1, 0), (0, 1), (0, -1), (1, 1), (1, -1), (-1, 1), (-1, -1)]
OWN_BATCH, LIST_BATCH = 16, 8
GROUP = 64
HOP = 17


def thirds(value):
    high = value.astype(jnp.bfloat16).astype(jnp.float32)
    rest = value - high
    middle = rest.astype(jnp.bfloat16).astype(jnp.float32)
    return [high, middle, rest - middle]


class Plan:
    def __init__(self, size_x, size_y, depth, slots, width):
        self.size_x, self.size_y, self.depth = size_x, size_y, depth
        self.slots, self.width = slots, width
        self.markers = slots * width

        def cap(reach, size):
            return -(-2 * reach * self.markers // size // width) * width

        corner = width // 4
        self.caps = [cap(2, size_x), cap(1, size_x), cap(2, size_y), cap(1, size_y)] + [corner] * 4
        self.starts = [sum(self.caps[:d]) for d in range(8)]
        self.listed = sum(self.caps)
        self.faces = self.starts[4]
        self.tiles = slots + self.listed // width
        self.total = self.tiles * width
        self.tile_rows = -(-self.tiles // 8) * 8
        self.outers = (size_x + 2) // 2 + 2
        self.outer_rows = 2 * (depth + 4)
        self.grid_rows = self.outers * self.outer_rows

    def span(self, d):
        if d < 4:
            return self.starts[d], self.caps[d]
        return self.faces, self.width


def row_mask(shape, value):
    return lax.broadcasted_iota(jnp.int32, shape, 0) == value


def prepare(plan, data, first, count, batch, spots, own, plain, places):
    width, size_y = plan.width, plan.size_y
    f32, bf16 = jnp.float32, jnp.bfloat16
    k_row = lax.broadcasted_iota(jnp.int32, (32, 6 * width), 0)
    n_lane = lax.broadcasted_iota(jnp.int32, (32, 6 * width), 1)
    kind = k_row % 8
    part, inside = n_lane // width, n_lane % width
    hit = ((kind < 5) & (part == kind)) | ((kind > 4) & (part == 5) & (inside // size_y == kind - 5))
    select = jnp.where(hit & (k_row < 24), 1.0, 0.0).astype(bf16)
    k_row = lax.broadcasted_iota(jnp.int32, (32, 8 * width), 0)
    n_lane = lax.broadcasted_iota(jnp.int32, (32, 8 * width), 1)
    hit = (k_row % 8 == n_lane // width) & (k_row < 24)
    spread_out = jnp.where(hit, 1.0, 0.0).astype(bf16)
    step = 4
    for t0 in range(0, count, step):
        n = min(step, count - t0) * width
        d = data[:, t0 * width : t0 * width + n]
        at = slice((first + t0) * width, (first + t0) * width + n)
        rows = lax.broadcasted_iota(jnp.int32, (8, n), 0)
        w = stencil(jnp.where(rows < 3, d[0:8], 0.5))
        factors = jnp.concatenate([v[2:3] for v in w] + [v[0:1] for v in w], axis=0)
        stack = jnp.concatenate(thirds(factors) + [jnp.zeros((8, n), f32)], axis=0)
        left = stack.T.astype(bf16)
        base = (first + t0) * width * HOP
        x = [
            jnp.dot(left, spread_out[:, i * width : (i + 2) * width], preferred_element_type=f32)
            for i in (4, 6)
        ]
        x = [x[i // 2][:, (i % 2) * width : (i % 2 + 1) * width] for i in range(4)]
        for i in range(0, 4, 2):
            z = jnp.dot(left, spread_out[:, i * width : (i + 2) * width], preferred_element_type=f32)
            for j in range(2):
                for h in range(2):
                    for side in range(2):
                        row = base + 8 * h + 2 * (i + j) + side
                        value = z[:, j * width : (j + 1) * width] * x[2 * h + side]
                        spots[pl.ds(row, n, stride=HOP), :] = value
        block = jnp.concatenate([v[1:2] for v in w] + [d[7:8], d[3:6]], axis=0)
        stack = jnp.concatenate(thirds(block) + [jnp.zeros((8, n), f32)], axis=0).astype(bf16)
        wide = lax.dot_general(
            stack, select, (((0,), (0,)), ((), ())), preferred_element_type=f32
        )
        cols = [wide[:, i * width : (i + 1) * width] for i in range(6)]
        lane = lax.broadcasted_iota(jnp.int32, (n, width), 1)
        y = jnp.where(lane < 3 * size_y, lane % size_y, -1000).astype(f32)
        pattern = pick(y - cols[4] + 1.0, cols[:4])
        plain[at, :] = pattern
        own[at, :] = pattern * cols[5]
    keys, zs, bases, goods = [], [], [], []
    for t in range(count):
        at = slice(t * width, (t + 1) * width)
        bx = data[6:7, at].astype(jnp.int32)
        bz = data[8:9, at].astype(jnp.int32)
        good = data[9:10, at] > 0.0
        lane = lax.broadcasted_iota(jnp.int32, (1, width), 1)
        step_in = lane % batch
        across = bx + 2
        side, outer = across % 2, across // 2
        spare = plan.grid_rows + ((plan.size_x + 2) // 2) * plan.outer_rows + 8 * step_in
        base = side * plan.grid_rows + outer * plan.outer_rows + 2 * bz
        bases.append(jnp.where(good, base, spare))
        keys.append(jnp.where(good, side * (plan.outers + 8) + outer, -100 - 10 * step_in))
        zs.append(bz)
        goods.append(jnp.where(good, 1, 0))
    rows = -(-count // 8) * 8
    fill = [jnp.zeros((rows - count, width), jnp.int32)] if rows > count else []
    key, z = jnp.concatenate(keys + fill, axis=0), jnp.concatenate(zs + fill, axis=0)
    base = jnp.concatenate(bases + fill, axis=0)
    lane = lax.broadcasted_iota(jnp.int32, (rows, width), 1) % batch

    def near(a, b, most):
        return (a - b <= most) & (b - a <= most)

    clashes = [
        (lane >= d) & near(key, pltpu.roll(key, d, 1), 1) & near(z, pltpu.roll(z, d, 1), 3)
        for d in range(1, batch)
    ]
    second = clashes[0]
    for clash in clashes[1:]:
        second = second | clash
    second = jnp.where(second, 1, 0)
    bad = jnp.zeros((rows, width), jnp.int32)
    for d, clash in enumerate(clashes):
        both = second * pltpu.roll(second, d + 1, 1)
        bad = jnp.maximum(bad, jnp.where(clash, both, 0))
    places[first : first + rows, :] = base + second * (2 * plan.grid_rows)
    good = jnp.concatenate(goods + fill, axis=0)
    lane = lax.broadcasted_iota(jnp.int32, (rows, width), 1) // GROUP
    state = jnp.zeros((rows, width), jnp.int32)
    for h in range(width // GROUP):
        here = lane == h
        worst = jnp.max(jnp.where(here, bad, 0), axis=1, keepdims=True)
        some = jnp.max(jnp.where(here, good, 0), axis=1, keepdims=True)
        filled = jnp.sum(jnp.where(here, good, 0), axis=1, keepdims=True)
        state = jnp.where(here, some * (1 + worst * filled), state)
    below = plan.tile_rows + first
    places[below : below + rows, :] = state
    below = 2 * plan.tile_rows + first
    places[below : below + rows, :] = base


def place():
    nx, ny = lax.axis_size("gx"), lax.axis_size("gy")
    return nx, ny, lax.axis_index("gx"), lax.axis_index("gy")


def send_kernel(plan, *refs):
    arguments, tile_count = refs[:5], refs[5]
    (own, plain, spots, places, slot_map, any_over) = refs[6:12]
    data, one_hot, lists, inbox, corners, got, note, notes = refs[12:20]
    send_sem, recv_sem, note_send, note_recv, load_sem = refs[20:25]
    offsets, forces, base_x, base_y, base_z = refs[25:]
    loads = [
        pltpu.make_async_copy(far, near, load_sem.at[i])
        for i, (far, near) in enumerate(zip(arguments, refs[25:]))
    ]
    for load in loads:
        load.start()
    f32, bf16 = jnp.float32, jnp.bfloat16
    slots, width, markers = plan.slots, plan.width, plan.markers
    nx, ny, mx, my = place()
    devices = nx * ny
    me = mx * ny + my

    def other(i):
        to = lax.rem(me + i, devices)
        return to // ny, lax.rem(to, ny)

    barrier = pltpu.get_barrier_semaphore()

    def greet(i, carry):
        pl.semaphore_signal(barrier, inc=1, device_id=other(i), device_id_type=MESH)
        return carry

    lax.fori_loop(1, devices, greet, 0)
    for load in loads:
        load.wait()

    live = jnp.where(lax.broadcasted_iota(jnp.int32, (slots, width), 0) < tile_count[0], 1.0, 0.0)
    bx, by, bz = base_x[...], base_y[...], base_z[...]
    values = [offsets[c] for c in range(3)] + [forces[c] * live for c in range(3)]
    values = values + [bx.astype(f32), by.astype(f32), bz.astype(f32), live]
    data[10:16, :] = jnp.zeros((6, markers), f32)
    for k, value in enumerate(values):
        for t in range(slots):
            data[k : k + 1, t * width : (t + 1) * width] = value[t : t + 1, :]
    ahead_x = jnp.where(bx >= plan.size_x - 2, live, 0.0)
    back_x = jnp.where(bx < 1, live, 0.0)
    ahead_y = jnp.where(by >= plan.size_y - 2, 1.0, 0.0)
    back_y = jnp.where(by < 1, 1.0, 0.0)
    flags = []
    for step_x, step_y in WAYS:
        flag = {1: ahead_x, -1: back_x, 0: live}[step_x]
        flags.append(flag if step_y == 0 else flag * (ahead_y if step_y > 0 else back_y))
    flag = jnp.concatenate(flags, axis=0)
    lines = 8 * slots
    r, c = (lax.broadcasted_iota(jnp.int32, (width, width), a) for a in range(2))
    upper = jnp.where(r <= c, 1.0, 0.0).astype(bf16)
    r, c = (lax.broadcasted_iota(jnp.int32, (lines, lines), a) for a in range(2))
    before = jnp.where((c < r) & (c // slots == r // slots), 1.0, 0.0).astype(bf16)
    within = jnp.dot(flag.astype(bf16), upper, preferred_element_type=f32)
    count = jnp.broadcast_to(jnp.sum(flag, axis=1, keepdims=True), (lines, width))
    earlier = jnp.dot(before, count.astype(bf16), preferred_element_type=f32)
    slot = jnp.where(flag > 0.0, earlier + within - 1.0, -1.0)
    slot_map[...] = slot
    over = jnp.zeros((slots, width), f32)
    for d in range(8):
        here = slot[d * slots : (d + 1) * slots]
        over = jnp.maximum(over, jnp.where(here >= plan.caps[d], 1.0, 0.0))
    note[...] = jnp.broadcast_to(jnp.max(over), note.shape)
    fill_one_hot(plan, slot_map, one_hot)
    stack = jnp.concatenate(thirds(data[...]), axis=0).astype(bf16)
    found = lax.dot_general(
        stack, one_hot[...], (((1,), (1,)), ((), ())), preferred_element_type=f32
    )
    found = found[0:16] + found[16:32] + found[32:48]
    lane = lax.broadcasted_iota(jnp.int32, (1, plan.listed), 1)
    for row, axis, size in ((6, 0, plan.size_x), (7, 1, plan.size_y)):
        shift = jnp.zeros((1, plan.listed), f32)
        for d in range(8):
            inside = (lane >= plan.starts[d]) & (lane < plan.starts[d] + plan.caps[d])
            shift = jnp.where(inside, float(WAYS[d][axis] * size), shift)
        moved_by = jnp.where(row_mask((16, plan.listed), row), shift * found[9:10], 0.0)
        found = found - moved_by
    lists[...] = found

    pl.semaphore_wait(barrier, devices - 1)

    def word(i):
        return pltpu.make_async_remote_copy(
            src_ref=note,
            dst_ref=notes.at[i],
            send_sem=note_send.at[i],
            recv_sem=note_recv.at[i],
            device_id=other(i),
            device_id_type=MESH,
        )

    def tell(i, carry):
        word(i).start()
        return carry

    lax.fori_loop(1, devices, tell, 0)
    copies = []
    for d, (step_x, step_y) in enumerate(WAYS):
        start, size = plan.span(d)
        target = inbox.at[:, pl.ds(start, size)] if d < 4 else corners.at[d - 4]
        copies.append(
            pltpu.make_async_remote_copy(
                src_ref=lists.at[:, pl.ds(start, size)],
                dst_ref=target,
                send_sem=send_sem.at[d],
                recv_sem=recv_sem.at[d],
                device_id=(lax.rem(mx + step_x + nx, nx), lax.rem(my + step_y + ny, ny)),
                device_id_type=MESH,
            )
        )
        copies[-1].start()

    prepare(plan, data, 0, slots, OWN_BATCH, spots, own, plain, places)
    for copy in copies:
        copy.wait()

    got[:, 0 : plan.faces] = inbox[...]
    lane = lax.broadcasted_iota(jnp.int32, (16, width), 1) // plan.caps[4]
    last = corners[0]
    for i in range(1, 4):
        last = jnp.where(lane == i, corners[i], last)
    got[:, plan.faces :] = last
    prepare(plan, got, slots, plan.tiles - slots, LIST_BATCH, spots, own, plain, places)

    def hear(i, most):
        word(i).wait()
        return jnp.maximum(most, notes[i])

    any_over[0] = jnp.max(lax.fori_loop(1, devices, hear, note[...])).astype(jnp.int32)


def fill_one_hot(plan, slot_map, one_hot):
    for d in range(8):
        rows = plan.caps[d]
        index = lax.broadcasted_iota(jnp.int32, (rows, plan.width), 0).astype(jnp.float32)
        for t in range(plan.slots):
            line = slot_map[d * plan.slots + t : d * plan.slots + t + 1, :]
            hot = jnp.where(index == line, 1.0, 0.0).astype(jnp.bfloat16)
            one_hot[plan.starts[d] : plan.starts[d] + rows, t * plan.width : (t + 1) * plan.width] = hot


def main_kernel(plan, time_step, *refs):
    own, plain, spots, places, tile_count, u_in, density_in, u_out, velocity = refs[:9]
    grid, table, found, sums, u_s, density_s, sems = refs[9:]
    f32, bf16 = jnp.float32, jnp.bfloat16
    width, depth, size_y, total = plan.width, plan.depth, plan.size_y, plan.total
    outer_rows, grid_rows = plan.outer_rows, plan.grid_rows
    loads = [
        pltpu.make_async_copy(u_in, u_s, sems.at[0]),
        pltpu.make_async_copy(density_in, density_s, sems.at[1]),
    ]
    for load in loads:
        load.start()
    zero = jnp.zeros((8, width), f32)
    group = divisor(4 * grid_rows // 8, 52)

    def clear(i, carry):
        for j in range(group):
            grid[pl.ds(pl.multiple_of((i * group + j) * 8, 8), 8), :] = zero
        return carry

    lax.fori_loop(0, 4 * grid_rows // 8 // group, clear, 0)
    for o in (0, 1, plan.outers - 2, plan.outers - 1):
        for g in range(2):
            at = g * grid_rows + o * outer_rows
            table[at : at + outer_rows, :] = jnp.zeros((outer_rows, width), f32)
    found[plan.markers :, :] = jnp.zeros((plan.listed, width), f32)

    def spread_group(batch, g, carry):
        first = g * GROUP
        state = places[plan.tile_rows * width + first]

        def windows(j):
            here = places[first + j]
            at = first * HOP + j * HOP
            row = jnp.broadcast_to(own[pl.ds(first + j, 1), :], (8, width))
            one, two = pl.ds(here, 8), pl.ds(here + outer_rows, 8)
            return [
                (one, grid[one, :] + spots[pl.ds(at, 8), :] * row),
                (two, grid[two, :] + spots[pl.ds(at + 8, 8), :] * row),
            ]

        @pl.when(state == 1)
        def _():
            for j0 in range(0, GROUP, batch):
                stores = []
                for j in range(j0, j0 + batch):
                    stores = stores + windows(j)
                for where, value in stores:
                    grid[where, :] = value

        @pl.when(state > 1)
        def _():
            def single(j, c):
                for where, value in windows(j):
                    grid[where, :] = value
                return c

            lax.fori_loop(0, state - 1, single, 0)

        return carry

    live_groups = tile_count[0] * (width // GROUP)
    lists_from, all_groups = plan.markers // GROUP, total // GROUP
    lax.fori_loop(0, live_groups, functools.partial(spread_group, OWN_BATCH), 0)
    lax.fori_loop(lists_from, all_groups, functools.partial(spread_group, LIST_BATCH), 0)

    def fold(i, carry):
        at = i * outer_rows
        ends = [(2 * depth, 0, 2), (2, 2 * depth + 2, 4)]
        for to, source, rows in ends:
            grid[pl.ds(at + to, rows), :] = grid[pl.ds(at + to, rows), :] + grid[pl.ds(at + source, rows), :]
        return carry

    lax.fori_loop(0, 4 * plan.outers, fold, 0)
    for load in loads:
        load.wait()

    def lines(g, outer, side):
        return pl.ds(g * grid_rows + outer * outer_rows + 2 + side, depth, stride=2)

    def plane(p, homes):
        force = None
        for copy in range(2):
            for g, outer, side in homes:
                part = grid[lines(2 * copy + g, outer, side), :]
                force = part if force is None else force + part
        force = force.T
        scale = time_step / density_s[p]
        pieces = []
        for c in range(3):
            value = u_s[c, p] + force[c * size_y : (c + 1) * size_y] * scale
            u_s[c, p] = value
            pieces.append(value)
        if width > 3 * size_y:
            pieces.append(jnp.zeros((width - 3 * size_y, depth), f32))
        back = jnp.concatenate(pieces, axis=0).T
        for g, outer, side in homes:
            table[lines(g, outer, side), :] = back
            at = g * grid_rows + outer * outer_rows + side
            table[pl.ds(at, 1), :] = back[depth - 1 : depth]
            table[pl.ds(at + 2 * depth + 2, 1), :] = back[0:1]
            table[pl.ds(at + 2 * depth + 4, 1), :] = back[1:2]

    def pair(i, carry):
        plane(2 * i, [(0, i + 1, 1), (1, i + 1, 0)])
        plane(2 * i + 1, [(0, i + 2, 0), (1, i + 1, 1)])
        return carry

    lax.fori_loop(0, plan.size_x // 2, pair, 0)
    leave = pltpu.make_async_copy(u_s, u_out, sems.at[2])
    leave.start()

    def read_group(g, carry):
        first = g * GROUP

        @pl.when(places[plan.tile_rows * width + first] > 0)
        def _():
            for j in range(GROUP):
                here = places[2 * plan.tile_rows * width + first + j]
                at = first * HOP + j * HOP
                sums[9 * j : 9 * j + 8, :] = (
                    table[pl.ds(here, 8), :] * spots[pl.ds(at, 8), :]
                    + table[pl.ds(here + outer_rows, 8), :] * spots[pl.ds(at + 8, 8), :]
                )
            for j in range(0, GROUP, 8):
                row = sums[pl.ds(9 * j, 8, stride=9), :]
                for s in range(1, 8):
                    row = row + sums[pl.ds(9 * j + s, 8, stride=9), :]
                block = pl.ds(pl.multiple_of(first + j, 8), 8)
                found[block, :] = row * plain[block, :]

        return carry

    lax.fori_loop(0, live_groups, read_group, 0)
    lax.fori_loop(lists_from, all_groups, read_group, 0)
    r = lax.broadcasted_iota(jnp.int32, (16, width), 0)
    lane = lax.broadcasted_iota(jnp.int32, (16, width), 1)
    by_part = jnp.where((lane // size_y == r) & (lane < 3 * size_y), 1.0, 0.0).astype(bf16)
    block = 4 * width
    for first in range(0, total, block):
        n = min(block, total - first)
        value = found[first : first + n, :]
        result = None
        for piece in thirds(value):
            part = lax.dot_general(
                by_part, piece.astype(bf16), (((1,), (1,)), ((), ())), preferred_element_type=f32
            )
            result = part if result is None else result + part
        velocity[:, first : first + n] = result[0:8]
    leave.wait()


def return_kernel(plan, *refs):
    velocity, slot_map, tile_count, out, one_hot, inbox, corners, send_sem, recv_sem = refs
    f32, bf16 = jnp.float32, jnp.bfloat16
    width = plan.width
    nx, ny, mx, my = place()
    barrier = pltpu.get_barrier_semaphore()

    def neighbour(step_x, step_y):
        return (lax.rem(mx + step_x + nx, nx), lax.rem(my + step_y + ny, ny))

    for way in WAYS:
        pl.semaphore_signal(barrier, inc=1, device_id=neighbour(*way), device_id_type=MESH)
    pl.semaphore_wait(barrier, len(WAYS))
    copies = []
    for d, (step_x, step_y) in enumerate(WAYS):
        start, size = plan.span(d)
        target = inbox.at[:, pl.ds(start, size)] if d < 4 else corners.at[d - 4]
        copies.append(
            pltpu.make_async_remote_copy(
                src_ref=velocity.at[:, pl.ds(plan.markers + start, size)],
                dst_ref=target,
                send_sem=send_sem.at[d],
                recv_sem=recv_sem.at[d],
                device_id=neighbour(-step_x, -step_y),
                device_id_type=MESH,
            )
        )
        copies[-1].start()
    fill_one_hot(plan, slot_map, one_hot)
    for copy in copies:
        copy.wait()
    lane = lax.broadcasted_iota(jnp.int32, (8, width), 1) // plan.caps[4]
    last = corners[0]
    for i in range(1, 4):
        last = jnp.where(lane == i, corners[i], last)
    back = jnp.concatenate([inbox[...], last], axis=1)
    stack = jnp.concatenate(thirds(back) + [jnp.zeros_like(back)], axis=0).astype(bf16)
    extra = jnp.dot(stack, one_hot[...], preferred_element_type=f32)
    extra = extra[0:8] + extra[8:16] + extra[16:24]
    total = velocity[:, 0 : plan.markers] + extra
    live = tile_count[0]
    for t in range(plan.slots):
        row = total[:, t * width : (t + 1) * width]
        row = jnp.where(lax.broadcasted_iota(jnp.int32, row.shape, 0) * 0 + t < live, row, 0.0)
        for c in range(3):
            out[c, t : t + 1, :] = row[c : c + 1, :]


def on_device(u_old, density, offsets, forces, base_x, base_y, base_z, tile_count):
    time_step = 0.5
    _, size_x, size_y, depth = u_old.shape
    slots, width = base_x.shape
    plan = Plan(size_x, size_y, depth, slots, width)
    f32, bf16 = jnp.float32, jnp.bfloat16
    devices = lax.axis_size("gx") * lax.axis_size("gy")
    whole, scalars = pl.BlockSpec(memory_space=pltpu.VMEM), pl.BlockSpec(memory_space=pltpu.SMEM)
    far = pl.BlockSpec(memory_space=pl.ANY)
    lines = 8 * slots
    dma = pltpu.SemaphoreType.DMA
    own, plain, spots, places, slot_map, over = pl.pallas_call(
        functools.partial(send_kernel, plan),
        out_shape=[
            jax.ShapeDtypeStruct((plan.total, width), f32),
            jax.ShapeDtypeStruct((plan.total, width), f32),
            jax.ShapeDtypeStruct((plan.total * HOP, width), f32),
            jax.ShapeDtypeStruct((3 * plan.tile_rows, width), jnp.int32),
            jax.ShapeDtypeStruct((lines, width), f32),
            jax.ShapeDtypeStruct((1,), jnp.int32),
        ],
        in_specs=[far] * 5 + [scalars],
        out_specs=[whole] * 5 + [scalars],
        scratch_shapes=[
            pltpu.VMEM((16, plan.markers), f32),
            pltpu.VMEM((plan.listed, plan.markers), bf16),
            pltpu.VMEM((16, plan.listed), f32),
            pltpu.VMEM((16, plan.faces), f32),
            pltpu.VMEM((4, 16, width), f32),
            pltpu.VMEM((16, plan.listed), f32),
            pltpu.VMEM((8, width), f32),
            pltpu.VMEM((devices, 8, width), f32),
            dma((8,)),
            dma((8,)),
            dma((devices,)),
            dma((devices,)),
            dma((5,)),
        ]
        + [pltpu.VMEM(offsets.shape, f32)] * 2
        + [pltpu.VMEM(base_x.shape, jnp.int32)] * 3,
        compiler_params=pltpu.CompilerParams(
            vmem_limit_bytes=SEND_LIMIT, collective_id=0, has_side_effects=True
        ),
        name="send",
    )(offsets, forces, base_x, base_y, base_z, tile_count)

    def sparse(*args):
        u_new, velocity = pl.pallas_call(
            functools.partial(main_kernel, plan, time_step),
            out_shape=[
                jax.ShapeDtypeStruct(u_old.shape, f32),
                jax.ShapeDtypeStruct((8, plan.total), f32),
            ],
            in_specs=[whole] * 3 + [scalars] * 2 + [far] * 2,
            out_specs=[far, whole],
            scratch_shapes=[
                pltpu.VMEM((4 * plan.grid_rows, width), f32),
                pltpu.VMEM((2 * plan.grid_rows, width), f32),
                pltpu.VMEM((plan.total, width), f32),
                pltpu.VMEM((9 * GROUP, width), f32),
                pltpu.VMEM(u_old.shape, f32),
                pltpu.VMEM(density.shape, f32),
                dma((3,)),
            ],
            compiler_params=pltpu.CompilerParams(vmem_limit_bytes=MAIN_LIMIT),
            name="main",
        )(own, plain, spots, places.reshape(-1), tile_count, u_old, density)
        out = pl.pallas_call(
            functools.partial(return_kernel, plan),
            out_shape=jax.ShapeDtypeStruct((3, slots, width), f32),
            in_specs=[whole] * 2 + [scalars],
            out_specs=whole,
            scratch_shapes=[
                pltpu.VMEM((plan.listed, plan.markers), bf16),
                pltpu.VMEM((8, plan.faces), f32),
                pltpu.VMEM((4, 8, width), f32),
                dma((8,)),
                dma((8,)),
            ],
            compiler_params=pltpu.CompilerParams(
                vmem_limit_bytes=VMEM_LIMIT, collective_id=1, has_side_effects=True
            ),
            name="give_back",
        )(velocity, slot_map, tile_count)
        return u_new, out

    args = (u_old, density, offsets, forces, base_x, base_y, base_z, tile_count)
    return lax.cond(over[0] > 0, dense_device, sparse, *args)


def solution(mesh):
    in_specs = (
        P(None, "gx", "gy", None),
        P("gx", "gy", None),
        P(None, ("gx", "gy"), None),
        P(None, ("gx", "gy"), None),
        P(("gx", "gy"), None),
        P(("gx", "gy"), None),
        P(("gx", "gy"), None),
        P(("gx", "gy")),
    )
    out_specs = (P(None, "gx", "gy", None), P(None, ("gx", "gy"), None))
    return jax.shard_map(
        on_device, mesh=mesh, in_specs=in_specs, out_specs=out_specs, check_vma=False
    )
```

profile of v0, /device:TPU:0, one launch (start us, length us, event | category | flops | bytes accessed | tf_op | source)
XLA Modules:
  0.0 43.9 jit_solution(8872215874372236323)
XLA Ops:
  1.3 15.0 %send.1 = (f32[2944,128]{1,0:T(8,128)S(1)}, f32[2944,128]{1,0:T(8,128)S(1)}, f32[50048,128]{1,0:T(8,128)S(1)}, s32[72,128]{1,0:T(8,128)S(1)}, f32[128,128]{1,0:T(8,128)S(1)}, /*index=5*/s32[1]{0:T(128)}) custom-call(f32[3,16,128]{2,1,0:T(8,128)} %refs_0_.1, f32[3,16,128]{2,1,0:T(8,128)} %refs_1_.1, s32[16,128]{1,0:T(8,128)} %refs_2_.1, s32[16,128]{1,0:T(8,128)} %refs_3_.1, ...), custom_call_target="tpu_custom_call" | custom-call | tf_op jit(solution)/shard_map/send/pallas_call | solution.py:782
  16.9 26.5 %conditional.1 = (f32[3,32,32,256]{3,2,1,0:T(8,128)}, f32[3,16,128]{2,1,0:T(8,128)S(1)}) conditional(s32[]{:T(128)} %bitcast.23, (s32[72,128]{1,0:T(8,128)S(1)}, f32[2944,128]{1,0:T(8,128)S(1)}, f32[2944,128]{1,0:T(8,128)S(1)}, f32[50048,128]{1,0:T(8,128)S(1)}, s32[1]{0:T(128)}, /*index=5*/f32[3,32,32,256]{3,2,1,0:T(8,128)}, ...), branch_computations={%region_0.0_spmd, %region_1.0_spmd} | conditional | flops 26424655872 | bytes 72049816 | solution.py:858
  16.9 10.1 %main.1 = (f32[3,32,32,256]{3,2,1,0:T(8,128)}, f32[8,2944]{1,0:T(8,128)S(1)}) custom-call(f32[2944,128]{1,0:T(8,128)S(1)} %get-tuple-element.32.refs_0_, f32[2944,128]{1,0:T(8,128)S(1)} %get-tuple-element.33.refs_1_, f32[50048,128]{1,0:T(8,128)S(1)} %get-tuple-element.34.refs_2_, s32[9216]{0:T(1024)S(1)} %bitcast.54, s32[1]{0:T(128)} %get-tuple-element.36.refs_4_.refs_2_, ...), custom_call_target="tpu_custom_call" | custom-call | tf_op jit(solution)/shard_map/cond/branch_0_fun/main/pallas_call | solution.py:818
  27.0 0.0 copy-start
  27.0 0.6 %copy-done = f32[8,2944]{1,0:T(8,128)} copy-done((f32[8,2944]{1,0:T(8,128)}, f32[8,2944]{1,0:T(8,128)S(1)}, u32[]{:S(2)}) %copy-start) | copy-done | bytes 94232 | tf_op jit(solution)/shard_map/cond
  27.6 15.5 %give_back.1 = f32[3,16,128]{2,1,0:T(8,128)S(1)} custom-call(f32[8,2944]{1,0:T(8,128)} %copy-done, f32[128,128]{1,0:T(8,128)S(1)} %get-tuple-element.41.refs_1_, s32[1]{0:T(128)} %get-tuple-element.36.refs_4_.refs_2_), custom_call_target="tpu_custom_call" | custom-call | tf_op jit(solution)/shard_map/cond/branch_0_fun/give_back/pallas_call | solution.py:838
  43.3 0.6 %copy.36 = f32[3,16,128]{2,1,0:T(8,128)} copy(f32[3,16,128]{2,1,0:T(8,128)S(1)} %get-tuple-element.107) | data formatting | bytes 49152
Async XLA Ops:
  27.0 0.6 %copy-start = (f32[8,2944]{1,0:T(8,128)}, f32[8,2944]{1,0:T(8,128)S(1)}, u32[]{:S(2)}) copy-start(f32[8,2944]{1,0:T(8,128)S(1)} %get-tuple-element.40.refs_0_) | copy-start | bytes 282628 | tf_op jit(solution)/shard_map/cond
where the time goes:
time: 43.2 us; the launch traced here: 43.9 us
  Pallas kernels  40.5 us (94%)
  between operations  1.92 us (4%)
  local copies, waits for them, and re-layouts  1.23 us (3%)
    pallas_call x1, Pallas kernels, sparse(): pl.pallas_call(functools.partial(return_kernel, plan), out_shape=jax.Shap...  15.5 us
    pallas_call x1, Pallas kernels, on_device(): pl.pallas_call(functools.partial(send_kernel, plan), out_shape=[jax.Shape...  15 us
    pallas_call x1, Pallas kernels, sparse(): pl.pallas_call(functools.partial(main_kernel, plan, time_step), out_shape...  10.1 us

commit v1 on v0

--- a/solution.py
+++ b/solution.py
@@ -9,7 +9,7 @@
 
 VMEM_LIMIT = 60 * 1024 * 1024
 SEND_LIMIT = 10 * 1024 * 1024
-MAIN_LIMIT = 35 * 1024 * 1024
+MAIN_LIMIT = 26 * 1024 * 1024
 
 
 def divisor(count, most):
@@ -426,46 +426,9 @@
     return nx, ny, lax.axis_index("gx"), lax.axis_index("gy")
 
 
-def send_kernel(plan, *refs):
-    arguments, tile_count = refs[:5], refs[5]
-    (own, plain, spots, places, slot_map, any_over) = refs[6:12]
-    data, one_hot, lists, inbox, corners, got, note, notes = refs[12:20]
-    send_sem, recv_sem, note_send, note_recv, load_sem = refs[20:25]
-    offsets, forces, base_x, base_y, base_z = refs[25:]
-    loads = [
-        pltpu.make_async_copy(far, near, load_sem.at[i])
-        for i, (far, near) in enumerate(zip(arguments, refs[25:]))
-    ]
-    for load in loads:
-        load.start()
+def list_slots(plan, bx, by, live):
     f32, bf16 = jnp.float32, jnp.bfloat16
-    slots, width, markers = plan.slots, plan.width, plan.markers
-    nx, ny, mx, my = place()
-    devices = nx * ny
-    me = mx * ny + my
-
-    def other(i):
-        to = lax.rem(me + i, devices)
-        return to // ny, lax.rem(to, ny)
-
-    barrier = pltpu.get_barrier_semaphore()
-
-    def greet(i, carry):
-        pl.semaphore_signal(barrier, inc=1, device_id=other(i), device_id_type=MESH)
-        return carry
-
-    lax.fori_loop(1, devices, greet, 0)
-    for load in loads:
-        load.wait()
-
-    live = jnp.where(lax.broadcasted_iota(jnp.int32, (slots, width), 0) < tile_count[0], 1.0, 0.0)
-    bx, by, bz = base_x[...], base_y[...], base_z[...]
-    values = [offsets[c] for c in range(3)] + [forces[c] * live for c in range(3)]
-    values = values + [bx.astype(f32), by.astype(f32), bz.astype(f32), live]
-    data[10:16, :] = jnp.zeros((6, markers), f32)
-    for k, value in enumerate(values):
-        for t in range(slots):
-            data[k : k + 1, t * width : (t + 1) * width] = value[t : t + 1, :]
+    slots, width = plan.slots, plan.width
     ahead_x = jnp.where(bx >= plan.size_x - 2, live, 0.0)
     back_x = jnp.where(bx < 1, live, 0.0)
     ahead_y = jnp.where(by >= plan.size_y - 2, 1.0, 0.0)
@@ -484,6 +447,85 @@
     count = jnp.broadcast_to(jnp.sum(flag, axis=1, keepdims=True), (lines, width))
     earlier = jnp.dot(before, count.astype(bf16), preferred_element_type=f32)
     slot = jnp.where(flag > 0.0, earlier + within - 1.0, -1.0)
+    return slot
+
+
+def read_group(plan, places, table, spots, plain, sums, found, first, to):
+    for j in range(GROUP):
+        here = places[2 * plan.tile_rows * plan.width + first + j]
+        at = first * HOP + j * HOP
+        sums[9 * j : 9 * j + 8, :] = (
+            table[pl.ds(here, 8), :] * spots[pl.ds(at, 8), :]
+            + table[pl.ds(here + plan.outer_rows, 8), :] * spots[pl.ds(at + 8, 8), :]
+        )
+    for j in range(0, GROUP, 8):
+        row = sums[pl.ds(9 * j, 8, stride=9), :]
+        for s in range(1, 8):
+            row = row + sums[pl.ds(9 * j + s, 8, stride=9), :]
+        row = row * plain[pl.ds(pl.multiple_of(first + j, 8), 8), :]
+        found[pl.ds(pl.multiple_of(to + j, 8), 8), :] = row
+
+
+def component_sums(plan, found, count, out):
+    f32, bf16 = jnp.float32, jnp.bfloat16
+    width, size_y = plan.width, plan.size_y
+    r = lax.broadcasted_iota(jnp.int32, (16, width), 0)
+    lane = lax.broadcasted_iota(jnp.int32, (16, width), 1)
+    by_part = jnp.where((lane // size_y == r) & (lane < 3 * size_y), 1.0, 0.0).astype(bf16)
+    block = 2 * width
+    for first in range(0, count, block):
+        n = min(block, count - first)
+        value = found[first : first + n, :]
+        result = None
+        for piece in thirds(value):
+            part = lax.dot_general(
+                by_part, piece.astype(bf16), (((1,), (1,)), ((), ())), preferred_element_type=f32
+            )
+            result = part if result is None else result + part
+        out[:, first : first + n] = result[0:8]
+
+
+def send_kernel(plan, *refs):
+    arguments, tile_count = refs[:5], refs[5]
+    (own, plain, spots, places, any_over) = refs[6:11]
+    data, one_hot, lists, inbox, corners, got, note, notes, slot_map = refs[11:20]
+    send_sem, recv_sem, note_send, note_recv, load_sem = refs[20:25]
+    offsets, forces, base_x, base_y, base_z = refs[25:]
+    loads = [
+        pltpu.make_async_copy(far, near, load_sem.at[i])
+        for i, (far, near) in enumerate(zip(arguments, refs[25:]))
+    ]
+    for load in loads:
+        load.start()
+    f32, bf16 = jnp.float32, jnp.bfloat16
+    slots, width, markers = plan.slots, plan.width, plan.markers
+    nx, ny, mx, my = place()
+    devices = nx * ny
+    me = mx * ny + my
+
+    def other(i):
+        to = lax.rem(me + i, devices)
+        return to // ny, lax.rem(to, ny)
+
+    barrier = pltpu.get_barrier_semaphore()
+
+    def greet(i, carry):
+        pl.semaphore_signal(barrier, inc=1, device_id=other(i), device_id_type=MESH)
+        return carry
+
+    lax.fori_loop(1, devices, greet, 0)
+    for load in loads:
+        load.wait()
+
+    live = jnp.where(lax.broadcasted_iota(jnp.int32, (slots, width), 0) < tile_count[0], 1.0, 0.0)
+    bx, by, bz = base_x[...], base_y[...], base_z[...]
+    values = [offsets[c] for c in range(3)] + [forces[c] * live for c in range(3)]
+    values = values + [bx.astype(f32), by.astype(f32), bz.astype(f32), live]
+    data[10:16, :] = jnp.zeros((6, markers), f32)
+    for k, value in enumerate(values):
+        for t in range(slots):
+            data[k : k + 1, t * width : (t + 1) * width] = value[t : t + 1, :]
+    slot = list_slots(plan, bx, by, live)
     slot_map[...] = slot
     over = jnp.zeros((slots, width), f32)
     for d in range(8):
@@ -518,11 +560,6 @@
             device_id_type=MESH,
         )
 
-    def tell(i, carry):
-        word(i).start()
-        return carry
-
-    lax.fori_loop(1, devices, tell, 0)
     copies = []
     for d, (step_x, step_y) in enumerate(WAYS):
         start, size = plan.span(d)
@@ -539,6 +576,11 @@
         )
         copies[-1].start()
 
+    def tell(i, carry):
+        word(i).start()
+        return carry
+
+    lax.fori_loop(1, devices, tell, 0)
     prepare(plan, data, 0, slots, OWN_BATCH, spots, own, plain, places)
     for copy in copies:
         copy.wait()
@@ -569,8 +611,8 @@
 
 
 def main_kernel(plan, time_step, *refs):
-    own, plain, spots, places, tile_count, u_in, density_in, u_out, velocity = refs[:9]
-    grid, table, found, sums, u_s, density_s, sems = refs[9:]
+    own, plain, spots, places, tile_count, u_in, density_in, u_out, partial, table = refs[:10]
+    grid, found, sums, u_s, density_s, sems = refs[10:]
     f32, bf16 = jnp.float32, jnp.bfloat16
     width, depth, size_y, total = plan.width, plan.depth, plan.size_y, plan.total
     outer_rows, grid_rows = plan.outer_rows, plan.grid_rows
@@ -593,7 +635,7 @@
         for g in range(2):
             at = g * grid_rows + o * outer_rows
             table[at : at + outer_rows, :] = jnp.zeros((outer_rows, width), f32)
-    found[plan.markers :, :] = jnp.zeros((plan.listed, width), f32)
+    found[...] = jnp.zeros((plan.listed, width), f32)
 
     def spread_group(batch, g, carry):
         first = g * GROUP
@@ -672,56 +714,34 @@
             table[pl.ds(at + 2 * depth + 4, 1), :] = back[1:2]
 
     def pair(i, carry):
-        plane(2 * i, [(0, i + 1, 1), (1, i + 1, 0)])
-        plane(2 * i + 1, [(0, i + 2, 0), (1, i + 1, 1)])
+        for j in range(pairs):
+            o = i * pairs + j
+            plane(2 * o, [(0, o + 1, 1), (1, o + 1, 0)])
+            plane(2 * o + 1, [(0, o + 2, 0), (1, o + 1, 1)])
         return carry
 
-    lax.fori_loop(0, plan.size_x // 2, pair, 0)
+    pairs = divisor(plan.size_x // 2, 2)
+    lax.fori_loop(0, plan.size_x // 2 // pairs, pair, 0)
     leave = pltpu.make_async_copy(u_s, u_out, sems.at[2])
     leave.start()
 
-    def read_group(g, carry):
+    def read_list(g, carry):
         first = g * GROUP
 
         @pl.when(places[plan.tile_rows * width + first] > 0)
         def _():
-            for j in range(GROUP):
-                here = places[2 * plan.tile_rows * width + first + j]
-                at = first * HOP + j * HOP
-                sums[9 * j : 9 * j + 8, :] = (
-                    table[pl.ds(here, 8), :] * spots[pl.ds(at, 8), :]
-                    + table[pl.ds(here + outer_rows, 8), :] * spots[pl.ds(at + 8, 8), :]
-                )
-            for j in range(0, GROUP, 8):
-                row = sums[pl.ds(9 * j, 8, stride=9), :]
-                for s in range(1, 8):
-                    row = row + sums[pl.ds(9 * j + s, 8, stride=9), :]
-                block = pl.ds(pl.multiple_of(first + j, 8), 8)
-                found[block, :] = row * plain[block, :]
+            read_group(plan, places, table, spots, plain, sums, found, first, first - plan.markers)
 
         return carry
 
-    lax.fori_loop(0, live_groups, read_group, 0)
-    lax.fori_loop(lists_from, all_groups, read_group, 0)
-    r = lax.broadcasted_iota(jnp.int32, (16, width), 0)
-    lane = lax.broadcasted_iota(jnp.int32, (16, width), 1)
-    by_part = jnp.where((lane // size_y == r) & (lane < 3 * size_y), 1.0, 0.0).astype(bf16)
-    block = 4 * width
-    for first in range(0, total, block):
-        n = min(block, total - first)
-        value = found[first : first + n, :]
-        result = None
-        for piece in thirds(value):
-            part = lax.dot_general(
-                by_part, piece.astype(bf16), (((1,), (1,)), ((), ())), preferred_element_type=f32
-            )
-            result = part if result is None else result + part
-        velocity[:, first : first + n] = result[0:8]
+    lax.fori_loop(lists_from, all_groups, read_list, 0)
+    component_sums(plan, found, plan.listed, partial)
     leave.wait()
 
 
 def return_kernel(plan, *refs):
-    velocity, slot_map, tile_count, out, one_hot, inbox, corners, send_sem, recv_sem = refs
+    partial, plain, spots, table, base_x, base_y, places, tile_count, out = refs[:9]
+    slot_map, one_hot, found, sums, velocity, inbox, corners, send_sem, recv_sem = refs[9:]
     f32, bf16 = jnp.float32, jnp.bfloat16
     width = plan.width
     nx, ny, mx, my = place()
@@ -739,7 +759,7 @@
         target = inbox.at[:, pl.ds(start, size)] if d < 4 else corners.at[d - 4]
         copies.append(
             pltpu.make_async_remote_copy(
-                src_ref=velocity.at[:, pl.ds(plan.markers + start, size)],
+                src_ref=partial.at[:, pl.ds(start, size)],
                 dst_ref=target,
                 send_sem=send_sem.at[d],
                 recv_sem=recv_sem.at[d],
@@ -748,6 +768,17 @@
             )
         )
         copies[-1].start()
+
+    def read(g, carry):
+        first = g * GROUP
+        read_group(plan, places, table, spots, plain, sums, found, first, first)
+        return carry
+
+    lax.fori_loop(0, plan.markers // GROUP, read, 0)
+    component_sums(plan, found, plan.markers, velocity)
+    shape = (plan.slots, width)
+    live = jnp.where(lax.broadcasted_iota(jnp.int32, shape, 0) < tile_count[0], 1.0, 0.0)
+    slot_map[...] = list_slots(plan, base_x[...], base_y[...], live)
     fill_one_hot(plan, slot_map, one_hot)
     for copy in copies:
         copy.wait()
@@ -759,7 +790,7 @@
     stack = jnp.concatenate(thirds(back) + [jnp.zeros_like(back)], axis=0).astype(bf16)
     extra = jnp.dot(stack, one_hot[...], preferred_element_type=f32)
     extra = extra[0:8] + extra[8:16] + extra[16:24]
-    total = velocity[:, 0 : plan.markers] + extra
+    total = velocity[...] + extra
     live = tile_count[0]
     for t in range(plan.slots):
         row = total[:, t * width : (t + 1) * width]
@@ -779,18 +810,17 @@
     far = pl.BlockSpec(memory_space=pl.ANY)
     lines = 8 * slots
     dma = pltpu.SemaphoreType.DMA
-    own, plain, spots, places, slot_map, over = pl.pallas_call(
+    own, plain, spots, places, over = pl.pallas_call(
         functools.partial(send_kernel, plan),
         out_shape=[
             jax.ShapeDtypeStruct((plan.total, width), f32),
             jax.ShapeDtypeStruct((plan.total, width), f32),
             jax.ShapeDtypeStruct((plan.total * HOP, width), f32),
             jax.ShapeDtypeStruct((3 * plan.tile_rows, width), jnp.int32),
-            jax.ShapeDtypeStruct((lines, width), f32),
             jax.ShapeDtypeStruct((1,), jnp.int32),
         ],
         in_specs=[far] * 5 + [scalars],
-        out_specs=[whole] * 5 + [scalars],
+        out_specs=[whole] * 4 + [scalars],
         scratch_shapes=[
             pltpu.VMEM((16, plan.markers), f32),
             pltpu.VMEM((plan.listed, plan.markers), bf16),
@@ -800,6 +830,7 @@
             pltpu.VMEM((16, plan.listed), f32),
             pltpu.VMEM((8, width), f32),
             pltpu.VMEM((devices, 8, width), f32),
+            pltpu.VMEM((lines, width), f32),
             dma((8,)),
             dma((8,)),
             dma((devices,)),
@@ -815,18 +846,19 @@
     )(offsets, forces, base_x, base_y, base_z, tile_count)
 
     def sparse(*args):
-        u_new, velocity = pl.pallas_call(
+        places_line = places.reshape(-1)
+        u_new, partial, table = pl.pallas_call(
             functools.partial(main_kernel, plan, time_step),
             out_shape=[
                 jax.ShapeDtypeStruct(u_old.shape, f32),
-                jax.ShapeDtypeStruct((8, plan.total), f32),
+                jax.ShapeDtypeStruct((8, plan.listed), f32),
+                jax.ShapeDtypeStruct((2 * plan.grid_rows, width), f32),
             ],
             in_specs=[whole] * 3 + [scalars] * 2 + [far] * 2,
-            out_specs=[far, whole],
+            out_specs=[far, whole, whole],
             scratch_shapes=[
                 pltpu.VMEM((4 * plan.grid_rows, width), f32),
-                pltpu.VMEM((2 * plan.grid_rows, width), f32),
-                pltpu.VMEM((plan.total, width), f32),
+                pltpu.VMEM((plan.listed, width), f32),
                 pltpu.VMEM((9 * GROUP, width), f32),
                 pltpu.VMEM(u_old.shape, f32),
                 pltpu.VMEM(density.shape, f32),
@@ -834,24 +866,28 @@
             ],
             compiler_params=pltpu.CompilerParams(vmem_limit_bytes=MAIN_LIMIT),
             name="main",
-        )(own, plain, spots, places.reshape(-1), tile_count, u_old, density)
+        )(own, plain, spots, places_line, tile_count, u_old, density)
         out = pl.pallas_call(
             functools.partial(return_kernel, plan),
             out_shape=jax.ShapeDtypeStruct((3, slots, width), f32),
-            in_specs=[whole] * 2 + [scalars],
+            in_specs=[whole] * 6 + [scalars] * 2,
             out_specs=whole,
             scratch_shapes=[
+                pltpu.VMEM((lines, width), f32),
                 pltpu.VMEM((plan.listed, plan.markers), bf16),
+                pltpu.VMEM((plan.markers, width), f32),
+                pltpu.VMEM((9 * GROUP, width), f32),
+                pltpu.VMEM((8, plan.markers), f32),
                 pltpu.VMEM((8, plan.faces), f32),
                 pltpu.VMEM((4, 8, width), f32),
                 dma((8,)),
                 dma((8,)),
             ],
             compiler_params=pltpu.CompilerParams(
-                vmem_limit_bytes=VMEM_LIMIT, collective_id=1, has_side_effects=True
+                vmem_limit_bytes=SEND_LIMIT, collective_id=1, has_side_effects=True
             ),
             name="give_back",
-        )(velocity, slot_map, tile_count)
+        )(partial, plain, spots, table, base_x, base_y, places_line, tile_count)
         return u_new, out
 
     args = (u_old, density, offsets, forces, base_x, base_y, base_z, tile_count)

time: 43.2 us -> 39.8 us (0.921); the launches traced: 43.9 us -> 39.8 us
  Pallas kernels: 40.5 us -> 37 us
  local copies, waits for them, and re-layouts: 1.23 us -> 0.62 us
    pallas_call x1, Pallas kernels: 15.5 us -> 11.5 us  [sparse(): pl.pallas_call(functools.partial(return_kernel, plan), out_shape=jax.Shap...]
    pallas_call x1, Pallas kernels: 10.1 us -> 11.1 us  [sparse(): pl.pallas_call(functools.partial(main_kernel, plan, time_step), out_shape...]
    pallas_call x1, Pallas kernels: 15 us -> 14.3 us  [on_device(): pl.pallas_call(functools.partial(send_kernel, plan), out_shape=[jax.Shape...]
    cond x2 -> x4, local copies, waits for them, and re-layouts: 0.62 us -> 0.01 us
where the time goes in v1:
time: 39.8 us
  Pallas kernels  37 us (93%)
  between operations  1.91 us (5%)
  local copies, waits for them, and re-layouts  0.62 us (2%)
    pallas_call x1, Pallas kernels, on_device(): pl.pallas_call(functools.partial(send_kernel, plan), out_shape=[jax.Shape...  14.3 us
    pallas_call x1, Pallas kernels, sparse(): pl.pallas_call(functools.partial(return_kernel, plan), out_shape=jax.Shap...  11.5 us
    pallas_call x1, Pallas kernels, sparse(): pl.pallas_call(functools.partial(main_kernel, plan, time_step), out_shape...  11.1 us

profile of v1, /device:TPU:0, one launch (start us, length us, event | category | flops | bytes accessed | tf_op | source)
XLA Modules:
  0.0 39.8 jit_solution(708888513169670944)
XLA Ops:
  1.3 14.3 %send.1 = (f32[2944,128]{1,0:T(8,128)S(1)}, f32[2944,128]{1,0:T(8,128)S(1)}, f32[50048,128]{1,0:T(8,128)S(1)}, s32[72,128]{1,0:T(8,128)S(1)}, s32[1]{0:T(128)}) custom-call(f32[3,16,128]{2,1,0:T(8,128)} %refs_0_.1, f32[3,16,128]{2,1,0:T(8,128)} %refs_1_.1, s32[16,128]{1,0:T(8,128)} %refs_2_.1, s32[16,128]{1,0:T(8,128)} %refs_3_.1, s32[16,128]{1,0:T(8,128)} %refs_4_.1, ...), custom_call_target="tpu_custom_call" | custom-call | tf_op jit(solution)/shard_map/send/pallas_call | solution.py:813
  16.2 22.9 %conditional.1 = (f32[3,32,32,256]{3,2,1,0:T(8,128)}, f32[3,16,128]{2,1,0:T(8,128)S(1)}) conditional(s32[]{:T(128)} %bitcast.23, (s32[72,128]{1,0:T(8,128)S(1)}, f32[2944,128]{1,0:T(8,128)S(1)}, f32[2944,128]{1,0:T(8,128)S(1)}, f32[50048,128]{1,0:T(8,128)S(1)}, s32[1]{0:T(128)}, /*index=5*/f32[3,32,32,256]{3,2,1,0:T(8,128)}, ...), branch_computations={%region_0.0_spmd, %region_1.0_spmd} | conditional | flops 26424655872 | bytes 72049816 | solution.py:894
  16.2 0.0 copy-start.5
  16.3 0.0 copy-start.7
  16.3 11.1 %main.1 = (f32[3,32,32,256]{3,2,1,0:T(8,128)}, f32[8,896]{1,0:T(8,128)S(1)}, f32[19760,128]{1,0:T(8,128)S(1)}) custom-call(f32[2944,128]{1,0:T(8,128)S(1)} %get-tuple-element.34.refs_0_, f32[2944,128]{1,0:T(8,128)S(1)} %get-tuple-element.35.refs_1_, f32[50048,128]{1,0:T(8,128)S(1)} %get-tuple-element.36.refs_2_, s32[9216]{0:T(1024)S(1)} %bitcast.52, ...), custom_call_target="tpu_custom_call" | custom-call | tf_op jit(solution)/shard_map/cond/branch_0_fun/main/pallas_call | solution.py:850
  27.4 0.0 copy-done.5
  27.4 0.0 copy-done.7
  27.4 11.5 %give_back.1 = f32[3,16,128]{2,1,0:T(8,128)S(1)} custom-call(f32[8,896]{1,0:T(8,128)S(1)} %get-tuple-element.42.refs_0_, f32[2944,128]{1,0:T(8,128)S(1)} %get-tuple-element.35.refs_1_, f32[50048,128]{1,0:T(8,128)S(1)} %get-tuple-element.36.refs_2_, f32[19760,128]{1,0:T(8,128)S(1)} %get-tuple-element.43.refs_3_, s32[16,128]{1,0:T(8,128)S(1)} %copy-done.5, ...), custom_call_target="tpu_custom_call" | custom-call | tf_op jit(solution)/shard_map/cond/branch_0_fun/give_back/pallas_call | solution.py:870
  39.2 0.6 %copy.36 = f32[3,16,128]{2,1,0:T(8,128)} copy(f32[3,16,128]{2,1,0:T(8,128)S(1)} %get-tuple-element.109) | data formatting | bytes 49152
Async XLA Ops:
  16.2 11.2 %copy-start.5 = (s32[16,128]{1,0:T(8,128)S(1)}, s32[16,128]{1,0:T(8,128)}, u32[]{:S(2)}) copy-start(s32[16,128]{1,0:T(8,128)} %get-tuple-element.44.refs_4_) | copy-start | bytes 24580 | tf_op jit(solution)/shard_map/cond
  16.3 11.2 %copy-start.7 = (s32[16,128]{1,0:T(8,128)S(1)}, s32[16,128]{1,0:T(8,128)}, u32[]{:S(2)}) copy-start(s32[16,128]{1,0:T(8,128)} %get-tuple-element.45.refs_5_) | copy-start | bytes 24580 | tf_op jit(solution)/shard_map/cond
